TPU v7x, 512 devices: a whole 4x8x8 slice. The times are simulated.
512 devices in a mesh: band: 8 (over x, core), domain: 64 (over y, z).
Axes of the slice: x: 4, y: 8, z: 8, core: 2. Of those that a mesh axis runs over, the one named last changes fastest.
Arguments:
- dens_part: float32 [8, 171, 147456], P('band', None, 'domain'), may hold values from -3 to 3
- counts: int32 [64], P('domain'), may hold values from 1 to 2304, 49152 in all
- gaunt: float32 [171, 525], replicated, may hold values from -0.4375 to 0.4375
- pair_waves: float32 [21, 400], replicated, may hold values from -1.25 to 1.25
- y_table: float32 [25, 50], replicated, may hold values from -1.25 to 1.25
- core: float32 [400], replicated, may hold values from 1 to 4
- radial_weights: float32 [400], replicated, may hold values from 0.0001 to 0.001
Outputs:
- dh_packed: float32 [171, 147456], P(None, 'domain')
- atom_energy: float32 [147456], P('domain')
Inputs may be any that keep to these rules, and one draw needn't show every extreme that they name: `counts`: atoms owned by each domain; they sum to 49152, and some domain owns exactly 2304.
All inputs are finite; a program needn't handle non-finite values. No bound on the sum of `counts` on one device may be relied on, other than what follows from the above.
Results may differ from a plain program's by a relative error of at most 0.0003.
Values sent between devices are 32-bit elements; how exact they have to be, the bound alone decides.
No kernel may reach another device: no remote copies, remote signals or barrier semaphores. Data moves between devices by JAX's collectives and lax.ppermute only.
A program may use at most 128 MiB of HBM per device.

v0:
```python
import functools

import jax
import jax.numpy as jnp
from jax import lax
from jax.experimental import pallas as pl
from jax.experimental.pallas import tpu as pltpu
from jax.sharding import PartitionSpec as P

highest = lax.Precision.HIGHEST
LANES = 128
QROWS = 32
PROWS = 192
GROUP = 14
RADIUS = 0.6203504908994
SLOPE = 0.44 * RADIUS / 3.0 / 7.8**2
SLOPE_SHIFT = 0.5 * (0.44 / 7.8) / SLOPE
SLOPE_REST = 0.9847450218426965 / SLOPE - SLOPE_SHIFT**2
ENERGY = 0.44 / 7.8
ENERGY_SHIFT = 0.7385587663820224 / ENERGY


def halves(x):
    high = x.astype(jnp.bfloat16)
    return high, (x - high.astype(jnp.float32)).astype(jnp.bfloat16)


def dot(a, b):
    return jnp.dot(a, b, preferred_element_type=jnp.float32)


def point_terms(points):
    log = jnp.log2(points * points + 0.25)
    t = jnp.exp2(log * (1.0 / 6.0))
    square = t * t
    share = 1.0 / (t + RADIUS / 7.8)
    energy = (square * square) * (share + ENERGY_SHIFT)
    shifted = share + SLOPE_SHIFT
    return energy, (points * (1.0 / square)) * (shifted * shifted + SLOPE_REST)


def evaluate_blocks(pairs, part_of, b_ref, c_ref, e_ref, lhs_p_ref, lhs_b_ref, p_refs, v_refs):
    grid_rows = lhs_p_ref.shape[0]
    cut = 208
    steps = [slice(0, 64), slice(64, 128), slice(128, 208), slice(208, 272), slice(272, 336), slice(336, 400)]

    def point_rhs(g):
        pieces = b_ref[pl.ds(2 * g, 2)]
        high, low = halves(jnp.concatenate([pieces[0], pieces[1]], axis=1))
        return jnp.concatenate([high, low, high], axis=0)

    def back(cols, high, low):
        first = dot(lhs_b_ref[:, cols], high)
        total = first[:QROWS] + first[QROWS:] + dot(lhs_b_ref[:QROWS, cols], low)
        return jnp.stack([total[:, :LANES], total[:, LANES:]])

    def finish(g, v_ref):
        c_ref[pl.ds(2 * g + 2, 2)] += back(slice(cut, grid_rows), v_ref[0, : grid_rows - cut, :], v_ref[1, : grid_rows - cut, :])

    def phase(g, now):
        other = 1 - now
        part = part_of(g)
        rhs = point_rhs(g + 1)
        finish(g - 1, v_refs[other])
        highs, lows = [], []
        for rows in steps:
            p_refs[other][rows, :] = dot(lhs_p_ref[rows, :], rhs)
            energy, potential = point_terms(p_refs[now][rows, :])
            e_ref[part, rows, :] += energy[:, :LANES] + energy[:, LANES:]
            high, low = halves(potential)
            if rows.stop <= cut:
                highs.append(high)
                lows.append(low)
                if rows.stop == cut:
                    c_ref[pl.ds(2 * g + 2, 2)] = back(
                        slice(0, cut), jnp.concatenate(highs, axis=0), jnp.concatenate(lows, axis=0)
                    )
            else:
                late = slice(rows.start - cut, rows.stop - cut)
                v_refs[now][0, late, :] = high
                v_refs[now][1, late, :] = low

    rhs = point_rhs(0)
    for rows in steps:
        p_refs[0][rows, :] = dot(lhs_p_ref[rows, :], rhs)

    def several(j, carry):
        for i in range(4):
            phase(4 * j + i, i % 2)
        return carry

    lax.fori_loop(0, pairs // 4, several, 0)
    for g in range(pairs // 4 * 4, pairs):
        phase(g, g % 2)
    finish(pairs - 1, v_refs[(pairs - 1) % 2])


def band_sum(recv_ref, rows):
    total = recv_ref[0, rows, :]
    for k in range(1, recv_ref.shape[0]):
        total = total + recv_ref[k, rows, :]
    return total


def row_pad(x, rows):
    return jnp.concatenate([x, jnp.zeros((rows - x.shape[0], x.shape[1]), jnp.float32)], axis=0)


def masked_density(total, live):
    rows = lax.broadcasted_iota(jnp.int32, total.shape, 0)
    density = jnp.where(live & (rows < 171), total, 0.0)
    return jnp.where((rows == 171) | (rows == 172), 1.0, density)


def energy_line(e_ref, part, weight_ref):
    return jnp.sum(e_ref[part] * weight_ref[...], axis=0, keepdims=True)


def forward(table, high, low):
    return dot(table, jnp.concatenate([high, high], axis=0)) + dot(table[:, :PROWS], low)


def wide_start(recv_ref, at, live, mt, mt_copy, b_ref, directions):
    total = row_pad(band_sum(recv_ref, slice(at, recv_ref.shape[1])), PROWS)
    dh, dl = halves(masked_density(total, live))
    mt_copy.wait()
    blocks = forward(mt[: directions * QROWS, :], dh, dl)
    b_ref[:directions] = blocks.reshape(directions, QROWS, LANES)


def wide_finish(c_ref, m_hl, live, directions):
    ch, cl = halves(c_ref[2 : 2 + directions].reshape(directions * QROWS, LANES))
    first = dot(m_hl[:, : directions * QROWS], ch)
    ham = first[:PROWS] + first[PROWS:] + dot(m_hl[:PROWS, : directions * QROWS], cl)
    return jnp.where(live, ham, 0.0)[:171]


def narrow_start(recv_ref, live, mt, b_ref, at):
    total = band_sum(recv_ref, slice(0, 48))
    pieces = [total[:, 32 * i : 32 * i + 32] for i in range(4)]
    spread = jnp.concatenate([jnp.concatenate([p] * 4, axis=1) for p in pieces], axis=0)
    density = masked_density(spread, live)
    lane_group = lax.broadcasted_iota(jnp.int32, density.shape, 1) // 32
    blocks = jnp.zeros((GROUP * QROWS, LANES), jnp.float32)
    for i in range(4):
        high, low = halves(jnp.where(lane_group == i, density, 0.0))
        rows = slice(i * GROUP * QROWS, (i + 1) * GROUP * QROWS)
        blocks = blocks + forward(mt[rows, :], high, low)
    b_ref[at : at + GROUP] = blocks.reshape(GROUP, QROWS, LANES)


def narrow_finish(c_ref, m_hl, line, live, at):
    ch, cl = halves(c_ref[at + 2 : at + 2 + GROUP].reshape(GROUP * QROWS, LANES))
    lanes = lax.broadcasted_iota(jnp.int32, (PROWS, LANES), 1) // 32
    ham = jnp.zeros((PROWS, LANES), jnp.float32)
    for i in range(4):
        cols = slice(i * GROUP * QROWS, (i + 1) * GROUP * QROWS)
        table = m_hl[:, cols]
        first = dot(table, ch)
        part = first[:PROWS] + first[PROWS:] + dot(table[:PROWS], cl)
        ham = ham + jnp.where(lanes == i, part, 0.0)
    rows = lax.broadcasted_iota(jnp.int32, (PROWS, LANES), 0)
    ham = jnp.where(rows == 171, line, ham)
    ham = sum(ham[:, 32 * i : 32 * i + 32] for i in range(4))
    packed = jnp.concatenate([ham[48 * i : 48 * i + 48] for i in range(4)], axis=1)
    return jnp.where(live, packed, 0.0)


def chunk_kernel(base, narrow_base, copies, directions, scal_ref, recv_ref, *refs):
    mt_far, m_far, lhs_p, lhs_b, weight = refs[:5]
    out_ref, b_ref, c_ref, e_ref, p0, p1, v0, v1, mt, m_hl, sem = refs[5:]
    mt_copy = pltpu.make_async_copy(mt_far, mt, sem.at[0])
    mt_copy.start()
    m_copy = pltpu.make_async_copy(m_far, m_hl, sem.at[1])
    m_copy.start()
    lane = lax.broadcasted_iota(jnp.int32, (1, LANES), 1)
    live = base + scal_ref[1] * LANES + lane < scal_ref[0]
    e_ref[...] = jnp.zeros_like(e_ref)
    wide_start(recv_ref, 0 if narrow_base is None else 48, live, mt, mt_copy, b_ref, directions)
    pairs, part_of = directions // 2, lambda g: 0
    if narrow_base is not None:
        narrow_live = narrow_base + scal_ref[1] * 32 + lane % 32 < scal_ref[0]
        narrow_start(recv_ref, narrow_live, mt, b_ref, directions)
        filled = pairs + (directions - 3 * GROUP) // 2
        part_of = lambda g, wide=pairs: (g >= wide).astype(jnp.int32) + (g >= filled).astype(jnp.int32) if not isinstance(g, int) else int(g >= wide) + int(g >= filled)
        pairs = pairs + GROUP // 2
    evaluate_blocks(pairs, part_of, b_ref, c_ref, e_ref, lhs_p, lhs_b, (p0, p1), (v0, v1))
    m_copy.wait()
    energy = jnp.where(live, energy_line(e_ref, 0, weight), 0.0)
    pieces = [jnp.broadcast_to(energy, (8, LANES))]
    if narrow_base is not None:
        line = energy_line(e_ref, 1, weight) + jnp.where(lane < 96, energy_line(e_ref, 2, weight), 0.0)
        pieces.append(narrow_finish(c_ref, m_hl, line, narrow_live, directions))
    pieces.append(wide_finish(c_ref, m_hl, live, directions))
    at = 0
    for piece in pieces:
        rows = slice(at, at + piece.shape[0])
        for k in range(copies):
            out_ref[k, rows, :] = piece
        at += piece.shape[0]


def chunk_call(base, narrow_base, copies, directions, scal, recv, tables):
    narrow = narrow_base is not None
    tables = [pltpu.with_memory_space_constraint(t, pltpu.HBM) for t in tables[:2]] + list(tables[2:])
    shape = (copies, 179 + 48 * narrow, LANES)
    blocks = directions + GROUP * narrow
    grid_rows = tables[2].shape[0]
    return pl.pallas_call(
        functools.partial(chunk_kernel, base, narrow_base, copies, directions),
        out_shape=jax.ShapeDtypeStruct(shape, jnp.float32),
        in_specs=[pl.BlockSpec(memory_space=pltpu.SMEM)]
        + [pl.BlockSpec(memory_space=pltpu.VMEM)]
        + [pl.BlockSpec(memory_space=pltpu.HBM)] * 2
        + [pl.BlockSpec(memory_space=pltpu.VMEM)] * 3,
        out_specs=pl.BlockSpec(memory_space=pltpu.VMEM),
        scratch_shapes=[pltpu.VMEM((blocks + 2, QROWS, LANES), jnp.float32)] * 2
        + [pltpu.VMEM((1 + 2 * narrow, grid_rows, LANES), jnp.float32)]
        + [pltpu.VMEM((grid_rows, 2 * LANES), jnp.float32)] * 2
        + [pltpu.VMEM((2, grid_rows, 2 * LANES), jnp.bfloat16)] * 2
        + [pltpu.VMEM(t.shape, jnp.bfloat16) for t in tables[:2]]
        + [pltpu.SemaphoreType.DMA((2,))],
        cost_estimate=pl.CostEstimate(flops=8_000_000_000, bytes_accessed=4_000_000, transcendentals=10_000_000),
        compiler_params=pltpu.CompilerParams(vmem_limit_bytes=18 * 1024 * 1024),
    )(scal, recv, *tables)


def table_kernel(gaunt_ref, waves_ref, y_ref, core_ref, rw_ref, mt_far, m_far, lhs_p, lhs_b, weight_ref, *scratch):
    gt_ref, mf_ref, mt_ref, m_hl, sem = scratch
    entries, columns = gaunt_ref.shape
    pairs, grid = waves_ref.shape
    harmonics, directions = y_ref.shape
    gt_pad = jnp.concatenate([gaunt_ref[...], jnp.zeros((256 - entries, columns), jnp.float32)], axis=0)
    gt_pad = jnp.concatenate([gt_pad, jnp.zeros((256, 640 - columns), jnp.float32)], axis=1)
    turned = gt_pad.T
    gt_ref[0] = turned[:, :LANES]
    gt_ref[1] = turned[:, LANES:]
    mf_ref[...] = jnp.zeros_like(mf_ref)
    for q in range(pairs):
        for half in range(2):
            part = gt_ref[half, pl.ds(q, harmonics, stride=pairs), :]
            made = lax.dot_general(
                y_ref[...], part, (((0,), (0,)), ((), ())), precision=highest, preferred_element_type=jnp.float32
            )
            mf_ref[half, pl.ds(q, directions, stride=QROWS), :] = made
    m = jnp.concatenate([mf_ref[0], mf_ref[1]], axis=1)
    mh, ml = halves(m.T[:PROWS])
    m_hl[:PROWS, :] = mh
    m_hl[PROWS:, :] = ml
    m_copy = pltpu.make_async_copy(m_hl, m_far, sem.at[0])
    m_copy.start()
    m = m[:, :PROWS]
    row = lax.broadcasted_iota(jnp.int32, m.shape, 0)
    col = lax.broadcasted_iota(jnp.int32, m.shape, 1)
    kind = row % QROWS
    unit = (row < directions * QROWS) & (((kind == 21) & (col == 171)) | ((kind == 22) & (col == 172)))
    high, low = halves(jnp.where(unit, 1.0, m))
    mt_ref[...] = jnp.concatenate([high, low], axis=1)
    mt_copy = pltpu.make_async_copy(mt_ref, mt_far, sem.at[1])
    mt_copy.start()
    waves = waves_ref[...]
    back = lambda x: x.astype(jnp.float32)
    wh = back(waves.astype(jnp.bfloat16))
    wl = waves - wh
    core = core_ref[...]
    ch = back(core.astype(jnp.bfloat16))
    cm = back((core - ch).astype(jnp.bfloat16))
    cl = core - ch - cm
    gap = lambda n: jnp.zeros((n, grid), jnp.float32)
    stack = jnp.concatenate(
        [wh, ch, cl, gap(QROWS - pairs - 2), wh, gap(QROWS - pairs), wl, cm, gap(QROWS - pairs - 1), gap(32)], axis=0
    )
    stack = jnp.concatenate([stack, jnp.zeros((LANES, 512 - grid), jnp.float32)], axis=1)
    lhs_p[...] = stack.T[:grid, :96].astype(jnp.bfloat16)
    weight = -(4.0 * jnp.pi / directions) * rw_ref[...]
    bh, bl = halves(jnp.concatenate([waves * (SLOPE * weight), gap(QROWS - pairs)], axis=0))
    lhs_b[...] = jnp.concatenate([bh, bl], axis=0)
    wide = jnp.concatenate([jnp.broadcast_to(ENERGY * weight, (LANES, grid)), jnp.zeros((LANES, 512 - grid), jnp.float32)], axis=1)
    weight_ref[...] = wide.T[:grid]
    m_copy.wait()
    mt_copy.wait()


def make_tables(gaunt, pair_waves, y_table, core, radial_weights):
    grid = core.shape[0]
    rows = 4 * GROUP * QROWS
    return pl.pallas_call(
        table_kernel,
        out_shape=(
            pltpu.HBM((rows, 2 * PROWS), jnp.bfloat16),
            pltpu.HBM((2 * PROWS, rows), jnp.bfloat16),
            jax.ShapeDtypeStruct((grid, 96), jnp.bfloat16),
            jax.ShapeDtypeStruct((2 * QROWS, grid), jnp.bfloat16),
            jax.ShapeDtypeStruct((grid, LANES), jnp.float32),
        ),
        in_specs=[pl.BlockSpec(memory_space=pltpu.VMEM)] * 5,
        out_specs=[pl.BlockSpec(memory_space=pltpu.HBM)] * 2 + [pl.BlockSpec(memory_space=pltpu.VMEM)] * 3,
        scratch_shapes=[
            pltpu.VMEM((2, 640, LANES), jnp.float32),
            pltpu.VMEM((2, rows, LANES), jnp.float32),
            pltpu.VMEM((rows, 2 * PROWS), jnp.bfloat16),
            pltpu.VMEM((2 * PROWS, rows), jnp.bfloat16),
            pltpu.SemaphoreType.DMA((2,)),
        ],
        cost_estimate=pl.CostEstimate(flops=2_000_000_000, bytes_accessed=4_000_000, transcendentals=0),
        compiler_params=pltpu.CompilerParams(vmem_limit_bytes=18 * 1024 * 1024),
    )(gaunt, pair_waves, y_table, core.reshape(1, grid), radial_weights.reshape(1, grid))


def send_a_kernel(block_ref, out_ref, sem):
    copies = [
        pltpu.make_async_copy(block_ref.at[:, 0, pl.ds(LANES * k, LANES)], out_ref.at[k], sem.at[k]) for k in range(8)
    ]
    for copy in copies:
        copy.start()
    for copy in copies:
        copy.wait()


def send_b_kernel(block_ref, out_ref, tail_ref, sem):
    entries = block_ref.shape[0]
    tail = pltpu.make_async_copy(block_ref.at[:, 0, pl.ds(2048, 256)], tail_ref, sem.at[8])
    tail.start()
    copies = [
        pltpu.make_async_copy(
            block_ref.at[:, 0, pl.ds(1024 + LANES * k, LANES)], out_ref.at[k, pl.ds(48, entries)], sem.at[k]
        )
        for k in range(8)
    ]
    for copy in copies:
        copy.start()
    tail.wait()
    rows = row_pad(tail_ref[...], PROWS)
    for k in range(8):
        own = rows[:, 32 * k : 32 * k + 32]
        out_ref[k, :48, :] = jnp.concatenate([own[48 * i : 48 * i + 48] for i in range(4)], axis=1)
    for copy in copies:
        copy.wait()


def send_call(kernel, rows, scratch, block):
    return pl.pallas_call(
        kernel,
        out_shape=jax.ShapeDtypeStruct((8, rows, LANES), jnp.float32),
        in_specs=[pl.BlockSpec(memory_space=pltpu.HBM)],
        out_specs=pl.BlockSpec(memory_space=pltpu.VMEM),
        scratch_shapes=scratch,
        cost_estimate=pl.CostEstimate(flops=100_000_000, bytes_accessed=1_500_000, transcendentals=0),
        compiler_params=pltpu.CompilerParams(vmem_limit_bytes=67_000_000),
    )(block)


def assemble_kernel(a_ref, b_ref, ham_ref, energy_ref, tail_ref, sem):
    copies = []
    for k in range(8):
        for part, ref, at in ((0, a_ref, 8), (1, b_ref, 56)):
            target = ham_ref.at[:, pl.ds(1024 * part + LANES * k, LANES)]
            copies.append(pltpu.make_async_copy(ref.at[k, pl.ds(at, 171)], target, sem.at[8 * part + k]))
    for copy in copies:
        copy.start()
    for i in range(4):
        rows = jnp.concatenate([b_ref[k, 8:56, 32 * i : 32 * i + 32] for k in range(8)], axis=1)
        if i < 3:
            tail_ref[48 * i : 48 * i + 48, :] = rows
        else:
            tail_ref[144:171, :] = rows[:27]
            energy_ref[16:18, :] = jnp.concatenate([rows[27:28, :LANES], rows[27:28, LANES:]], axis=0)
    tail = pltpu.make_async_copy(tail_ref, ham_ref.at[:, pl.ds(2048, 256)], sem.at[16])
    tail.start()
    for k in range(8):
        energy_ref[k : k + 1, :] = a_ref[k, 0:1, :]
        energy_ref[8 + k : 9 + k, :] = b_ref[k, 0:1, :]
    for copy in copies:
        copy.wait()
    tail.wait()


def assemble(all_a, all_b):
    return pl.pallas_call(
        assemble_kernel,
        out_shape=(jax.ShapeDtypeStruct((171, 2304), jnp.float32), jax.ShapeDtypeStruct((18, LANES), jnp.float32)),
        in_specs=[pl.BlockSpec(memory_space=pltpu.VMEM)] * 2,
        out_specs=[pl.BlockSpec(memory_space=pltpu.HBM), pl.BlockSpec(memory_space=pltpu.VMEM)],
        scratch_shapes=[pltpu.VMEM((171, 256), jnp.float32), pltpu.SemaphoreType.DMA((17,))],
        cost_estimate=pl.CostEstimate(flops=100_000_000, bytes_accessed=3_000_000, transcendentals=0),
        compiler_params=pltpu.CompilerParams(vmem_limit_bytes=8 * 1024 * 1024),
    )(all_a, all_b)


def per_device(dens_part, counts, gaunt, pair_waves, y_table, core, radial_weights):
    band_index = lax.axis_index("band").astype(jnp.int32)
    scal = jnp.stack([counts[0].astype(jnp.int32), band_index])
    directions = y_table.shape[1]
    rows = dens_part.transpose(1, 0, 2)
    send_a = send_call(send_a_kernel, 171, [pltpu.SemaphoreType.DMA((8,))], rows)
    recv_a = lax.all_to_all(send_a, "band", 0, 0, tiled=True)
    send_b = send_call(
        send_b_kernel, 219, [pltpu.VMEM((171, 256), jnp.float32), pltpu.SemaphoreType.DMA((9,))], rows
    )
    recv_b = lax.all_to_all(send_b, "band", 0, 0, tiled=True)
    tables = make_tables(gaunt, pair_waves, y_table, core, radial_weights)
    out_a = chunk_call(0, None, 8, directions, scal, recv_a, tables)
    all_a = lax.all_to_all(out_a, "band", 0, 0, tiled=True)
    out_b = chunk_call(1024, 2048, 1, directions, scal, recv_b, tables)
    all_b = lax.all_gather(out_b[0], "band", axis=0)
    ham, energy = assemble(all_a, all_b)
    return ham, energy.reshape(18 * LANES)


def solution(mesh):
    return jax.shard_map(
        per_device,
        mesh=mesh,
        in_specs=(P("band", None, "domain"), P("domain"), P(), P(), P(), P(), P()),
        out_specs=(P(None, "domain"), P("domain")),
        check_vma=False,
    )
```

profile of v0, /device:TPU:1, one launch (start us, length us, event | category | flops | bytes accessed | tf_op | source)
XLA Modules:
  0.0 79.8 jit_solution(1627069232033060234)
XLA Ops:
  0.6 2.2 %shard_map.86 = f32[8,171,128]{2,1,0:T(8,128)} custom-call(f32[171,1,2304]{2,1,0:T(1,128)} %bitcast.7), custom_call_target="tpu_custom_call" | custom-call | flops 100000000 | bytes 1500000 | tf_op jit(solution)/shard_map/pallas_call | solution.py:342
  2.8 10.9 %all-to-all-start = ((f32[8,171,128]{2,1,0:T(8,128)}), f32[8,171,128]{2,1,0:T(8,128)}, u32[]{:S(2)}, u32[]{:S(2)}) async-start(f32[8,171,128]{2,1,0:T(8,128)} %shard_map.86), calls=%async_computation | async-start | bytes 1441792 | tf_op jit(solution)/shard_map/all_to_all | solution.py:396
  13.8 0.0 copy-start.2
  13.8 0.0 copy-start.3
  13.8 0.0 copy-start.4
  14.5 2.3 %shard_map.89 = f32[8,219,128]{2,1,0:T(8,128)} custom-call(f32[171,1,2304]{2,1,0:T(1,128)} %bitcast.8), custom_call_target="tpu_custom_call" | custom-call | flops 100000000 | bytes 1500000 | tf_op jit(solution)/shard_map/pallas_call | solution.py:342
  16.8 0.0 copy-done.2
  16.8 0.0 copy-done.3
  16.8 0.0 copy-done.4
  16.8 0.0 copy-start
  16.8 1.0 %copy-done = f32[171,525]{1,0:T(8,128)S(1)} copy-done((f32[171,525]{1,0:T(8,128)S(1)}, f32[171,525]{1,0:T(8,128)}, u32[]{:S(2)}) %copy-start) | copy-done | bytes 359124
  17.9 0.0 copy-start.1
  17.9 0.8 copy-done.1
  18.7 5.3 %shard_map.87 = (bf16[1792,384]{1,0:T(8,128)(2,1)}, bf16[384,1792]{1,0:T(8,128)(2,1)}, bf16[400,96]{1,0:T(8,128)(2,1)S(1)}, bf16[64,400]{1,0:T(8,128)(2,1)S(1)}, f32[400,128]{1,0:T(8,128)S(1)}) custom-call(f32[171,525]{1,0:T(8,128)S(1)} %copy-done, f32[21,400]{1,0:T(8,128)S(1)} %copy-done.1, f32[25,50]{1,0:T(8,128)S(1)} %copy-done.2, f32[1,400]{1,0:T(1,128)S(1)} %bitcast.5, ...), custom_call_target="tpu_custom_call" | custom-call | flops 2000000000 | bytes 4000000 | tf_op jit(solution)/shard_map/pallas_call | solution.py:287
  23.9 1.4 %all-to-all-done.recv_ref = f32[8,171,128]{2,1,0:T(8,128)} async-done(((f32[8,171,128]{2,1,0:T(8,128)}), f32[8,171,128]{2,1,0:T(8,128)}, u32[]{:S(2)}, u32[]{:S(2)}) %all-to-all-start) | async-done | bytes 700448 | tf_op jit(solution)/shard_map/all_to_all | solution.py:396
  25.4 4.4 %all-to-all-start.2 = ((f32[8,219,128]{2,1,0:T(8,128)}), f32[8,219,128]{2,1,0:T(8,128)S(1)}, u32[]{:S(2)}, u32[]{:S(2)}) async-start(f32[8,219,128]{2,1,0:T(8,128)} %shard_map.89), calls=%async_computation.2 | async-start | bytes 1835008 | tf_op jit(solution)/shard_map/all_to_all | solution.py:400
  29.8 0.1 pad_add_fusion.scal_ref
  29.8 13.2 %shard_map.88 = f32[8,179,128]{2,1,0:T(8,128)} custom-call(s32[2]{0:T(128)S(1)} %pad_add_fusion.scal_ref, f32[8,171,128]{2,1,0:T(8,128)} %all-to-all-done.recv_ref, bf16[1792,384]{1,0:T(8,128)(2,1)} %get-tuple-element.9.refs_0_, bf16[384,1792]{1,0:T(8,128)(2,1)} %get-tuple-element.10.refs_1_, bf16[400,96]{1,0:T(8,128)(2,1)S(1)} %get-tuple-element.11.refs_2_, ...), custom_call_target="tpu_custom_call" | custom-call | flops 8000000000 | bytes 4000000 | tf_op jit(solution)/shard_map/pallas_call | solution.py:209
  43.1 0.3 all-to-all-done.2.recv_ref
  43.4 4.6 %all-to-all-start.1 = ((f32[8,179,128]{2,1,0:T(8,128)}), f32[8,179,128]{2,1,0:T(8,128)S(1)}, u32[]{:S(2)}, u32[]{:S(2)}) async-start(f32[8,179,128]{2,1,0:T(8,128)} %shard_map.88), calls=%async_computation.1 | async-start | bytes 1507328 | tf_op jit(solution)/shard_map/all_to_all | solution.py:403
  47.9 15.7 %shard_map.90 = f32[1,227,128]{2,1,0:T(8,128)S(1)} custom-call(s32[2]{0:T(128)S(1)} %pad_add_fusion.scal_ref, f32[8,219,128]{2,1,0:T(8,128)S(1)} %all-to-all-done.2.recv_ref, bf16[1792,384]{1,0:T(8,128)(2,1)} %get-tuple-element.9.refs_0_, bf16[384,1792]{1,0:T(8,128)(2,1)} %get-tuple-element.10.refs_1_, bf16[400,96]{1,0:T(8,128)(2,1)S(1)} %get-tuple-element.11.refs_2_, ...), custom_call_target="tpu_custom_call" | custom-call | flops 8000000000 | bytes 4000000 | tf_op jit(solution)/shard_map/pallas_call | solution.py:209
  63.6 14.2 %all_gather.3.b_ref = f32[8,227,128]{2,1,0:T(8,128)S(1)} all-gather(f32[1,227,128]{2,1,0:T(8,128)S(1)} %shard_map.90), channel_id=1, replica_groups=mesh['band'=8,'domain'=64] {'band'}, dimensions={0}, use_global_device_ids=true | all-gather | bytes 1046016 | tf_op jit(solution)/shard_map/all_gather | solution.py:405
  77.9 0.0 all-to-all-done.1.a_ref
  77.9 1.9 %shard_map.91 = (f32[171,2304]{1,0:T(8,128)}, f32[18,128]{1,0:T(8,128)}) custom-call(f32[8,179,128]{2,1,0:T(8,128)S(1)} %all-to-all-done.1.a_ref, f32[8,227,128]{2,1,0:T(8,128)S(1)} %all_gather.3.b_ref), custom_call_target="tpu_custom_call" | custom-call | flops 100000000 | bytes 3000000 | tf_op jit(solution)/shard_map/pallas_call | solution.py:379
Async XLA Ops:
  2.8 22.5 %all-to-all-start = ((f32[8,171,128]{2,1,0:T(8,128)}), f32[8,171,128]{2,1,0:T(8,128)}, u32[]{:S(2)}, u32[]{:S(2)}) async-start(f32[8,171,128]{2,1,0:T(8,128)} %shard_map.86), calls=%async_computation | async-start | bytes 1441792 | tf_op jit(solution)/shard_map/all_to_all | solution.py:396
  13.8 3.0 %copy-start.2 = (f32[25,50]{1,0:T(8,128)S(1)}, f32[25,50]{1,0:T(8,128)}, u32[]{:S(2)}) copy-start(f32[25,50]{1,0:T(8,128)} %y_ref.1) | copy-start | bytes 15004
  13.8 3.1 %copy-start.3 = (f32[400]{0:T(512)S(1)}, f32[400]{0:T(512)}, u32[]{:S(2)}) copy-start(f32[400]{0:T(512)} %param.12) | copy-start | bytes 4804
  13.8 3.1 %copy-start.4 = (f32[400]{0:T(512)S(1)}, f32[400]{0:T(512)}, u32[]{:S(2)}) copy-start(f32[400]{0:T(512)} %param.13) | copy-start | bytes 4804
  16.8 1.0 %copy-start = (f32[171,525]{1,0:T(8,128)S(1)}, f32[171,525]{1,0:T(8,128)}, u32[]{:S(2)}) copy-start(f32[171,525]{1,0:T(8,128)} %gaunt_ref.1) | copy-start | bytes 1077304
  17.9 0.8 %copy-start.1 = (f32[21,400]{1,0:T(8,128)S(1)}, f32[21,400]{1,0:T(8,128)}, u32[]{:S(2)}) copy-start(f32[21,400]{1,0:T(8,128)} %waves_ref.1) | copy-start | bytes 100804
  25.4 18.0 %all-to-all-start.2 = ((f32[8,219,128]{2,1,0:T(8,128)}), f32[8,219,128]{2,1,0:T(8,128)S(1)}, u32[]{:S(2)}, u32[]{:S(2)}) async-start(f32[8,219,128]{2,1,0:T(8,128)} %shard_map.89), calls=%async_computation.2 | async-start | bytes 1835008 | tf_op jit(solution)/shard_map/all_to_all | solution.py:400
  43.4 34.5 %all-to-all-start.1 = ((f32[8,179,128]{2,1,0:T(8,128)}), f32[8,179,128]{2,1,0:T(8,128)S(1)}, u32[]{:S(2)}, u32[]{:S(2)}) async-start(f32[8,179,128]{2,1,0:T(8,128)} %shard_map.88), calls=%async_computation.1 | async-start | bytes 1507328 | tf_op jit(solution)/shard_map/all_to_all | solution.py:403
where the time goes:
time: 80.5 us; the launch traced here: 79.8 us
  Pallas kernels  40.7 us (51%)
  starting transfers between devices  19.9 us (25%)
  blocking collectives  14.2 us (18%)
  local copies, waits for them, and re-layouts  1.82 us (2%)
  waiting for transfers between devices  1.68 us (2%)
  between operations  1.4 us (2%)
    pallas_call x2, Pallas kernels, chunk_call(): pl.pallas_call(functools.partial(chunk_kernel, base, narrow_base, copies,...  28.9 us
    all_gather x1, blocking collectives, per_device(): all_b = lax.all_gather(out_b[0], 'band', axis=0)  14.2 us
    all_to_all x1, starting transfers between devices, per_device(): recv_a = lax.all_to_all(send_a, 'band', 0, 0, tiled=True)  10.9 us
    pallas_call x1, Pallas kernels, make_tables(): pl.pallas_call(table_kernel, out_shape=(pltpu.HBM((rows, 2 * PROWS), jnp....  5.29 us
    all_to_all x1, starting transfers between devices, per_device(): all_a = lax.all_to_all(out_a, 'band', 0, 0, tiled=True)  4.57 us
    pallas_call x2, Pallas kernels, send_call(): pl.pallas_call(kernel, out_shape=jax.ShapeDtypeStruct((8, rows, LANES), j...  4.53 us
    all_to_all x1, starting transfers between devices, per_device(): recv_b = lax.all_to_all(send_b, 'band', 0, 0, tiled=True)  4.42 us
    pallas_call x1, Pallas kernels, assemble(): pl.pallas_call(assemble_kernel, out_shape=(jax.ShapeDtypeStruct((171, 230...  1.94 us
  transfers between devices with their start and end apart: 3, of which 2 were waited for; matrix products, arithmetic and copies ran while one was open for 0% of the time, Pallas kernels for 46%

commit v1 on v0

v1 whole, which is shorter than its diff:
```python
import functools

import jax
import jax.numpy as jnp
from jax import lax
from jax.experimental import pallas as pl
from jax.experimental.pallas import tpu as pltpu
from jax.sharding import PartitionSpec as P

highest = lax.Precision.HIGHEST
LANES = 128
QROWS = 32
PROWS = 192
GROUP = 14
RADIUS = 0.6203504908994
SLOPE = 0.44 * RADIUS / 3.0 / 7.8**2
SLOPE_SHIFT = 0.5 * (0.44 / 7.8) / SLOPE
SLOPE_REST = 0.9847450218426965 / SLOPE - SLOPE_SHIFT**2
ENERGY = 0.44 / 7.8
ENERGY_SHIFT = 0.7385587663820224 / ENERGY


def halves(x):
    high = x.astype(jnp.bfloat16)
    return high, (x - high.astype(jnp.float32)).astype(jnp.bfloat16)


def dot(a, b):
    return jnp.dot(a, b, preferred_element_type=jnp.float32)


def point_terms(points):
    log = jnp.log2(points * points + 0.25)
    t = jnp.exp2(log * (1.0 / 6.0))
    square = t * t
    share = 1.0 / (t + RADIUS / 7.8)
    energy = (square * square) * (share + ENERGY_SHIFT)
    shifted = share + SLOPE_SHIFT
    return energy, (points * (1.0 / square)) * (shifted * shifted + SLOPE_REST)


def evaluate_blocks(pairs, part_of, b_ref, c_ref, e_ref, lhs_p_ref, lhs_b_ref, p_refs, v_refs):
    grid_rows = lhs_p_ref.shape[0]
    cut = 208
    steps = [slice(0, 64), slice(64, 128), slice(128, 208), slice(208, 272), slice(272, 336), slice(336, 400)]

    def point_rhs(g):
        pieces = b_ref[pl.ds(2 * g, 2)]
        high, low = halves(jnp.concatenate([pieces[0], pieces[1]], axis=1))
        return jnp.concatenate([high, low, high], axis=0)

    def back(cols, high, low):
        first = dot(lhs_b_ref[:, cols], high)
        total = first[:QROWS] + first[QROWS:] + dot(lhs_b_ref[:QROWS, cols], low)
        return jnp.stack([total[:, :LANES], total[:, LANES:]])

    def finish(g, v_ref):
        c_ref[pl.ds(2 * g + 2, 2)] += back(slice(cut, grid_rows), v_ref[0, : grid_rows - cut, :], v_ref[1, : grid_rows - cut, :])

    def phase(g, now):
        other = 1 - now
        part = part_of(g)
        rhs = point_rhs(g + 1)
        finish(g - 1, v_refs[other])
        highs, lows = [], []
        for rows in steps:
            p_refs[other][rows, :] = dot(lhs_p_ref[rows, :], rhs)
            energy, potential = point_terms(p_refs[now][rows, :])
            e_ref[part, rows, :] += energy[:, :LANES] + energy[:, LANES:]
            high, low = halves(potential)
            if rows.stop <= cut:
                highs.append(high)
                lows.append(low)
                if rows.stop == cut:
                    c_ref[pl.ds(2 * g + 2, 2)] = back(
                        slice(0, cut), jnp.concatenate(highs, axis=0), jnp.concatenate(lows, axis=0)
                    )
            else:
                late = slice(rows.start - cut, rows.stop - cut)
                v_refs[now][0, late, :] = high
                v_refs[now][1, late, :] = low

    rhs = point_rhs(0)
    for rows in steps:
        p_refs[0][rows, :] = dot(lhs_p_ref[rows, :], rhs)

    def several(j, carry):
        for i in range(4):
            phase(4 * j + i, i % 2)
        return carry

    lax.fori_loop(0, pairs // 4, several, 0)
    for g in range(pairs // 4 * 4, pairs):
        phase(g, g % 2)
    finish(pairs - 1, v_refs[(pairs - 1) % 2])


def band_sum(recv_ref, rows):
    total = recv_ref[0, rows, :]
    for k in range(1, recv_ref.shape[0]):
        total = total + recv_ref[k, rows, :]
    return total


def row_pad(x, rows):
    return jnp.concatenate([x, jnp.zeros((rows - x.shape[0], x.shape[1]), jnp.float32)], axis=0)


def masked_density(total, live):
    rows = lax.broadcasted_iota(jnp.int32, total.shape, 0)
    density = jnp.where(live & (rows < 171), total, 0.0)
    return jnp.where((rows == 171) | (rows == 172), 1.0, density)


def energy_line(e_ref, part, weight_ref):
    return jnp.sum(e_ref[part] * weight_ref[...], axis=0, keepdims=True)


def forward(table, high, low):
    return dot(table, jnp.concatenate([high, high], axis=0)) + dot(table[:, :PROWS], low)


def start_blocks(recv_ref, lives, mt, b_ref, directions):
    lead = 48 * (len(lives) - 1)
    density = masked_density(row_pad(band_sum(recv_ref, slice(lead, recv_ref.shape[1])), PROWS), lives[0])
    if lead:
        total = band_sum(recv_ref, slice(0, lead))
        pieces = [total[:, 32 * i : 32 * i + 32] for i in range(4)]
        spread = jnp.concatenate([jnp.concatenate([p] * 4, axis=1) for p in pieces], axis=0)
        density = jnp.concatenate([density, masked_density(spread, lives[1])], axis=1)
    rows = directions * QROWS
    table = mt[...] if lead else mt[:rows, :]
    blocks = forward(table, *halves(density))
    b_ref[:directions] = blocks[:rows, :LANES].reshape(directions, QROWS, LANES)
    if lead:
        parts = blocks[:, LANES:].reshape(4, GROUP * QROWS, LANES)
        lane_group = lax.broadcasted_iota(jnp.int32, parts.shape[1:], 1) // 32
        chosen = parts[3]
        for i in range(3):
            chosen = jnp.where(lane_group == i, parts[i], chosen)
        b_ref[directions : directions + GROUP] = chosen.reshape(GROUP, QROWS, LANES)


def finish_blocks(c_ref, m_hl, lives, line, directions):
    rows = directions * QROWS
    sums = c_ref[2 : 2 + directions].reshape(rows, LANES)
    table = m_hl[:, :rows]
    if len(lives) > 1:
        table = m_hl[...]
        narrow = c_ref[directions + 2 : directions + 2 + GROUP].reshape(GROUP * QROWS, LANES)
        lane_group = lax.broadcasted_iota(jnp.int32, narrow.shape, 1) // 32
        spread = jnp.concatenate([jnp.where(lane_group == i, narrow, 0.0) for i in range(4)], axis=0)
        sums = jnp.concatenate([row_pad(sums, table.shape[1]), spread], axis=1)
    high, low = halves(sums)
    first = dot(table, high)
    ham = first[:PROWS] + first[PROWS:] + dot(table[:PROWS], low)
    wide = jnp.where(lives[0], ham[:171, :LANES], 0.0)
    if len(lives) == 1:
        return [wide]
    ham = ham[:, LANES:]
    kind = lax.broadcasted_iota(jnp.int32, (PROWS, LANES), 0)
    ham = jnp.where(kind == 171, line, ham)
    ham = sum(ham[:, 32 * i : 32 * i + 32] for i in range(4))
    packed = jnp.concatenate([ham[48 * i : 48 * i + 48] for i in range(4)], axis=1)
    return [jnp.where(lives[1], packed, 0.0), wide]


def chunk_kernel(base, narrow_base, copies, directions, owned_ref, recv_ref, *refs):
    mt, m_far, lhs_p, lhs_b, weight = refs[:5]
    out_ref, b_ref, c_ref, e_ref, p0, p1, v0, v1, m_hl, near_ref, sem = refs[5:]
    m_copy = pltpu.make_async_copy(m_far, m_hl, sem.at[copies])
    m_copy.start()
    lane = lax.broadcasted_iota(jnp.int32, (1, LANES), 1)
    lives = [base + lane < owned_ref[0:1, :]]
    pairs, part_of = directions // 2, lambda g: 0
    if narrow_base is not None:
        lives.append(narrow_base + lane % 32 < owned_ref[1:2, :])
        wide, filled = pairs, pairs + (directions - 3 * GROUP) // 2
        part_of = lambda g: jnp.where(g >= wide, 1, 0) + jnp.where(g >= filled, 1, 0)
        pairs = pairs + GROUP // 2
    e_ref[...] = jnp.zeros_like(e_ref)
    start_blocks(recv_ref, lives, mt, b_ref, directions)
    evaluate_blocks(pairs, part_of, b_ref, c_ref, e_ref, lhs_p, lhs_b, (p0, p1), (v0, v1))
    energy = jnp.where(lives[0], energy_line(e_ref, 0, weight), 0.0)
    line = None
    if narrow_base is not None:
        line = energy_line(e_ref, 1, weight) + jnp.where(lane < 96, energy_line(e_ref, 2, weight), 0.0)
    m_copy.wait()
    target = near_ref if copies > 1 else out_ref.at[0]
    at = 0
    for piece in [jnp.broadcast_to(energy, (8, LANES))] + finish_blocks(c_ref, m_hl, lives, line, directions):
        target[at : at + piece.shape[0], :] = piece
        at += piece.shape[0]
    if copies > 1:
        leaving = [pltpu.make_async_copy(near_ref, out_ref.at[k], sem.at[k]) for k in range(copies)]
        for copy in leaving:
            copy.start()
        for copy in leaving:
            copy.wait()


def chunk_call(base, narrow_base, copies, directions, owned, recv, tables):
    narrow = narrow_base is not None
    tables = [tables[0], pltpu.with_memory_space_constraint(tables[1], pltpu.HBM)] + list(tables[2:])
    shape = (copies, 179 + 48 * narrow, LANES)
    blocks = directions + GROUP * narrow
    grid_rows = tables[2].shape[0]
    return pl.pallas_call(
        functools.partial(chunk_kernel, base, narrow_base, copies, directions),
        out_shape=(pltpu.VMEM if copies == 1 else pltpu.HBM)(shape, jnp.float32),
        in_specs=[pl.BlockSpec(memory_space=pltpu.VMEM)] * 3
        + [pl.BlockSpec(memory_space=pltpu.HBM)]
        + [pl.BlockSpec(memory_space=pltpu.VMEM)] * 3,
        out_specs=pl.BlockSpec(memory_space=pltpu.VMEM if copies == 1 else pltpu.HBM),
        scratch_shapes=[pltpu.VMEM((blocks + 2, QROWS, LANES), jnp.float32)] * 2
        + [pltpu.VMEM((1 + 2 * narrow, grid_rows, LANES), jnp.float32)]
        + [pltpu.VMEM((grid_rows, 2 * LANES), jnp.float32)] * 2
        + [pltpu.VMEM((2, grid_rows, 2 * LANES), jnp.bfloat16)] * 2
        + [pltpu.VMEM(tables[1].shape, jnp.bfloat16)]
        + [pltpu.VMEM(shape[1:], jnp.float32), pltpu.SemaphoreType.DMA((copies + 1,))],
        cost_estimate=pl.CostEstimate(flops=8_000_000_000, bytes_accessed=4_000_000, transcendentals=10_000_000),
        compiler_params=pltpu.CompilerParams(vmem_limit_bytes=18 * 1024 * 1024),
    )(owned, recv, *tables)


def table_kernel(gaunt_ref, waves_ref, y_ref, core_ref, rw_ref, mt_ref, m_far, lhs_p, lhs_b, weight_ref, *scratch):
    gt_ref, mf_ref, m_hl, sem = scratch
    entries, columns = gaunt_ref.shape
    pairs, grid = waves_ref.shape
    harmonics, directions = y_ref.shape
    gt_pad = jnp.concatenate([gaunt_ref[...], jnp.zeros((256 - entries, columns), jnp.float32)], axis=0)
    gt_pad = jnp.concatenate([gt_pad, jnp.zeros((256, 640 - columns), jnp.float32)], axis=1)
    turned = gt_pad.T
    gt_ref[0] = turned[:, :LANES]
    gt_ref[1] = turned[:, LANES:]
    mf_ref[...] = jnp.zeros_like(mf_ref)
    for q in range(pairs):
        for half in range(2):
            part = gt_ref[half, pl.ds(q, harmonics, stride=pairs), :]
            made = lax.dot_general(
                y_ref[...], part, (((0,), (0,)), ((), ())), precision=highest, preferred_element_type=jnp.float32
            )
            mf_ref[half, pl.ds(q, directions, stride=QROWS), :] = made
    m = jnp.concatenate([mf_ref[0], mf_ref[1]], axis=1)
    mh, ml = halves(m.T[:PROWS])
    m_hl[:PROWS, :] = mh
    m_hl[PROWS:, :] = ml
    m_copy = pltpu.make_async_copy(m_hl, m_far, sem.at[0])
    m_copy.start()
    m = m[:, :PROWS]
    row = lax.broadcasted_iota(jnp.int32, m.shape, 0)
    col = lax.broadcasted_iota(jnp.int32, m.shape, 1)
    kind = row % QROWS
    unit = (row < directions * QROWS) & (((kind == 21) & (col == 171)) | ((kind == 22) & (col == 172)))
    high, low = halves(jnp.where(unit, 1.0, m))
    mt_ref[...] = jnp.concatenate([high, low], axis=1)
    waves = waves_ref[...]
    back = lambda x: x.astype(jnp.float32)
    wh = back(waves.astype(jnp.bfloat16))
    wl = waves - wh
    core = core_ref[...]
    ch = back(core.astype(jnp.bfloat16))
    cm = back((core - ch).astype(jnp.bfloat16))
    cl = core - ch - cm
    gap = lambda n: jnp.zeros((n, grid), jnp.float32)
    stack = jnp.concatenate(
        [wh, ch, cl, gap(QROWS - pairs - 2), wh, gap(QROWS - pairs), wl, cm, gap(QROWS - pairs - 1), gap(32)], axis=0
    )
    stack = jnp.concatenate([stack, jnp.zeros((LANES, 512 - grid), jnp.float32)], axis=1)
    lhs_p[...] = stack.T[:grid, :96].astype(jnp.bfloat16)
    weight = -(4.0 * jnp.pi / directions) * rw_ref[...]
    bh, bl = halves(jnp.concatenate([waves * (SLOPE * weight), gap(QROWS - pairs)], axis=0))
    lhs_b[...] = jnp.concatenate([bh, bl], axis=0)
    wide = jnp.concatenate([jnp.broadcast_to(ENERGY * weight, (LANES, grid)), jnp.zeros((LANES, 512 - grid), jnp.float32)], axis=1)
    weight_ref[...] = wide.T[:grid]
    m_copy.wait()


def make_tables(gaunt, pair_waves, y_table, core, radial_weights):
    grid = core.shape[0]
    rows = 4 * GROUP * QROWS
    return pl.pallas_call(
        table_kernel,
        out_shape=(
            jax.ShapeDtypeStruct((rows, 2 * PROWS), jnp.bfloat16),
            pltpu.HBM((2 * PROWS, rows), jnp.bfloat16),
            jax.ShapeDtypeStruct((grid, 96), jnp.bfloat16),
            jax.ShapeDtypeStruct((2 * QROWS, grid), jnp.bfloat16),
            jax.ShapeDtypeStruct((grid, LANES), jnp.float32),
        ),
        in_specs=[pl.BlockSpec(memory_space=pltpu.VMEM)] * 5,
        out_specs=[pl.BlockSpec(memory_space=pltpu.VMEM), pl.BlockSpec(memory_space=pltpu.HBM)]
        + [pl.BlockSpec(memory_space=pltpu.VMEM)] * 3,
        scratch_shapes=[
            pltpu.VMEM((2, 640, LANES), jnp.float32),
            pltpu.VMEM((2, rows, LANES), jnp.float32),
            pltpu.VMEM((2 * PROWS, rows), jnp.bfloat16),
            pltpu.SemaphoreType.DMA((1,)),
        ],
        cost_estimate=pl.CostEstimate(flops=2_000_000_000, bytes_accessed=4_000_000, transcendentals=0),
        compiler_params=pltpu.CompilerParams(vmem_limit_bytes=18 * 1024 * 1024),
    )(gaunt, pair_waves, y_table, core.reshape(1, grid), radial_weights.reshape(1, grid))


def send_kernel(first, narrow, block_ref, out_ref, near_ref, *scratch):
    entries = block_ref.shape[0]
    tail_ref, pack_ref, sem = scratch if narrow is not None else (None, None, *scratch)
    lead = 48 if narrow is not None else 0
    arrivals = [
        pltpu.make_async_copy(block_ref.at[:, 0, pl.ds(first + LANES * k, LANES)], near_ref.at[k], sem.at[k])
        for k in range(8)
    ]
    if narrow is not None:
        tail = pltpu.make_async_copy(block_ref.at[:, 0, pl.ds(narrow, 256)], tail_ref, sem.at[16])
        tail.start()
    for copy in arrivals:
        copy.start()
    leaving = []
    if narrow is not None:
        tail.wait()
        rows = row_pad(tail_ref[...], PROWS)
        for k in range(8):
            own = rows[:, 32 * k : 32 * k + 32]
            pack_ref[k] = jnp.concatenate([own[48 * i : 48 * i + 48] for i in range(4)], axis=1)
        leaving.append(pltpu.make_async_copy(pack_ref, out_ref.at[:, pl.ds(0, 48)], sem.at[17]))
        leaving[0].start()
    for k in range(8):
        arrivals[k].wait()
        copy = pltpu.make_async_copy(near_ref.at[k], out_ref.at[k, pl.ds(lead, entries)], sem.at[8 + k])
        copy.start()
        leaving.append(copy)
    for copy in leaving:
        copy.wait()


def send_call(first, narrow, rows):
    entries = rows.shape[0]
    scratch = [pltpu.VMEM((8, entries, LANES), jnp.float32)]
    if narrow is not None:
        scratch += [pltpu.VMEM((entries, 256), jnp.float32), pltpu.VMEM((8, 48, LANES), jnp.float32)]
    return pl.pallas_call(
        functools.partial(send_kernel, first, narrow),
        out_shape=pltpu.HBM((8, entries + (48 if narrow is not None else 0), LANES), jnp.float32),
        in_specs=[pl.BlockSpec(memory_space=pltpu.HBM)],
        out_specs=pl.BlockSpec(memory_space=pltpu.HBM),
        scratch_shapes=scratch + [pltpu.SemaphoreType.DMA((18,))],
        cost_estimate=pl.CostEstimate(flops=100_000_000, bytes_accessed=1_500_000, transcendentals=0),
        compiler_params=pltpu.CompilerParams(vmem_limit_bytes=6 * 1024 * 1024),
    )(rows)


def assemble_kernel(a_ref, b_ref, ham_ref, energy_far, tail_ref, energy_ref, sem):
    copies = []
    for k in range(8):
        for part, ref, at in ((0, a_ref, 56), (1, b_ref, 8)):
            target = ham_ref.at[:, pl.ds(1024 * part + LANES * k, LANES)]
            copies.append(pltpu.make_async_copy(ref.at[k, pl.ds(at, 171)], target, sem.at[8 * part + k]))
    for copy in copies:
        copy.start()
    for i in range(4):
        rows = jnp.concatenate([a_ref[k, 8:56, 32 * i : 32 * i + 32] for k in range(8)], axis=1)
        if i < 3:
            tail_ref[48 * i : 48 * i + 48, :] = rows
        else:
            tail_ref[144:171, :] = rows[:27]
            energy_ref[16:18, :] = jnp.concatenate([rows[27:28, :LANES], rows[27:28, LANES:]], axis=0)
    tail = pltpu.make_async_copy(tail_ref, ham_ref.at[:, pl.ds(2048, 256)], sem.at[16])
    tail.start()
    for k in range(8):
        energy_ref[k : k + 1, :] = a_ref[k, 0:1, :]
        energy_ref[8 + k : 9 + k, :] = b_ref[k, 0:1, :]
    energies = pltpu.make_async_copy(energy_ref, energy_far, sem.at[17])
    energies.start()
    for copy in copies:
        copy.wait()
    tail.wait()
    energies.wait()


def assemble(all_a, all_b):
    return pl.pallas_call(
        assemble_kernel,
        out_shape=(pltpu.HBM((171, 2304), jnp.float32), pltpu.HBM((18, LANES), jnp.float32)),
        in_specs=[pl.BlockSpec(memory_space=pltpu.VMEM)] * 2,
        out_specs=[pl.BlockSpec(memory_space=pltpu.HBM)] * 2,
        scratch_shapes=[
            pltpu.VMEM((171, 256), jnp.float32),
            pltpu.VMEM((18, LANES), jnp.float32),
            pltpu.SemaphoreType.DMA((18,)),
        ],
        cost_estimate=pl.CostEstimate(flops=100_000_000, bytes_accessed=3_000_000, transcendentals=0),
        compiler_params=pltpu.CompilerParams(vmem_limit_bytes=8 * 1024 * 1024),
    )(all_a, all_b)


def per_device(dens_part, counts, gaunt, pair_waves, y_table, core, radial_weights):
    band_index = lax.axis_index("band").astype(jnp.int32)
    widths = jnp.where(lax.broadcasted_iota(jnp.int32, (2, LANES), 0) == 0, LANES, 32)
    owned = counts[0].astype(jnp.int32) - band_index * widths
    directions = y_table.shape[1]
    rows = pltpu.with_memory_space_constraint(dens_part.transpose(1, 0, 2), pltpu.HBM)
    send_a = send_call(0, 2048, rows)
    recv_a = lax.all_to_all(send_a, "band", 0, 0, tiled=True)
    send_b = send_call(1024, None, rows)
    recv_b = lax.all_to_all(send_b, "band", 0, 0, tiled=True)
    tables = make_tables(gaunt, pair_waves, y_table, core, radial_weights)
    out_a = chunk_call(0, 2048, 8, directions, owned, recv_a, tables)
    all_a = lax.all_to_all(out_a, "band", 0, 0, tiled=True)
    out_b = chunk_call(1024, None, 1, directions, owned, recv_b, tables)
    all_b = lax.all_gather(out_b[0], "band", axis=0)
    ham, energy = assemble(all_a, all_b)
    return ham, energy.reshape(18 * LANES)


def solution(mesh):
    return jax.shard_map(
        per_device,
        mesh=mesh,
        in_specs=(P("band", None, "domain"), P("domain"), P(), P(), P(), P(), P()),
        out_specs=(P(None, "domain"), P("domain")),
        check_vma=False,
    )
```

time: 80.5 us -> 75.8 us (0.942)
  Pallas kernels: 40.7 us -> 34.3 us
  waiting for transfers between devices: 1.68 us -> 5.93 us
  local copies, waits for them, and re-layouts: 1.82 us -> 0.09 us
    pallas_call x2, Pallas kernels: 28.9 us -> 23.9 us  [chunk_call(): pl.pallas_call(functools.partial(chunk_kernel, base, narrow_base, copies,...]
    all_to_all x1, waiting for transfers between devices: 1.4 us -> 5.93 us  [per_device(): recv_a = lax.all_to_all(send_a, 'band', 0, 0, tiled=True)]
    unnamed x10, local copies, waits for them, and re-layouts: 1.82 us -> 0.02 us
    pallas_call x4, Pallas kernels: 11.8 us -> 10.4 us  [the longest x1 4.8 us: make_tables(): pl.pallas_call(table_kernel, out_shape=(jax.ShapeDtypeStruct((rows, 2 * P...]
  transfers between devices with their start and end apart: 3 -> 3, of which waited for: 2 -> 1; matrix products, arithmetic and copies ran while one was open for 0% -> 0% of each run, Pallas kernels for 46% -> 41%
where the time goes in v1:
time: 75.8 us; the launch traced here: 75.4 us
  Pallas kernels  34.3 us (45%)
  starting transfers between devices  19.5 us (26%)
  blocking collectives  14 us (18%)
  waiting for transfers between devices  5.93 us (8%)
  between operations  1.45 us (2%)
    pallas_call x2, Pallas kernels, chunk_call(): pl.pallas_call(functools.partial(chunk_kernel, base, narrow_base, copies,...  23.9 us
    all_gather x1, blocking collectives, per_device(): all_b = lax.all_gather(out_b[0], 'band', axis=0)  14 us
    all_to_all x1, starting transfers between devices, per_device(): recv_a = lax.all_to_all(send_a, 'band', 0, 0, tiled=True)  10.3 us
    all_to_all x1, waiting for transfers between devices, per_device(): recv_a = lax.all_to_all(send_a, 'band', 0, 0, tiled=True)  5.93 us
    all_to_all x1, starting transfers between devices, per_device(): all_a = lax.all_to_all(out_a, 'band', 0, 0, tiled=True)  4.83 us
    pallas_call x1, Pallas kernels, make_tables(): pl.pallas_call(table_kernel, out_shape=(jax.ShapeDtypeStruct((rows, 2 * P...  4.8 us
    all_to_all x1, starting transfers between devices, per_device(): recv_b = lax.all_to_all(send_b, 'band', 0, 0, tiled=True)  4.41 us
    pallas_call x2, Pallas kernels, send_call(): pl.pallas_call(functools.partial(send_kernel, first, narrow), out_shape=p...  4.29 us
  transfers between devices with their start and end apart: 3, of which 1 were waited for; matrix products, arithmetic and copies ran while one was open for 0% of the time, Pallas kernels for 41%

profile of v1, /device:TPU:1, one launch (start us, length us, event | category | flops | bytes accessed | tf_op | source)
XLA Modules:
  0.0 75.4 jit_solution(17225723692263110262)
XLA Ops:
  0.6 2.2 %shard_map.86 = f32[8,219,128]{2,1,0:T(8,128)} custom-call(f32[171,1,2304]{2,1,0:T(1,128)} %bitcast.8), custom_call_target="tpu_custom_call" | custom-call | flops 100000000 | bytes 1500000 | tf_op jit(solution)/shard_map/pallas_call | solution.py:341
  2.9 10.3 %all-to-all-start = ((f32[8,219,128]{2,1,0:T(8,128)}), f32[8,219,128]{2,1,0:T(8,128)S(1)}, u32[]{:S(2)}, u32[]{:S(2)}) async-start(f32[8,219,128]{2,1,0:T(8,128)} %shard_map.86), calls=%async_computation | async-start | bytes 1835008 | tf_op jit(solution)/shard_map/all_to_all | solution.py:403
  13.2 0.0 copy-start
  13.2 0.0 copy-start.1
  13.2 0.0 copy-start.2
  13.2 0.0 copy-start.3
  13.2 0.0 copy-start.4
  13.9 2.0 %shard_map.89 = f32[8,171,128]{2,1,0:T(8,128)} custom-call(f32[171,1,2304]{2,1,0:T(1,128)} %bitcast.9), custom_call_target="tpu_custom_call" | custom-call | flops 100000000 | bytes 1500000 | tf_op jit(solution)/shard_map/pallas_call | solution.py:341
  16.0 0.0 copy-done
  16.0 0.0 copy-done.1
  16.0 0.0 copy-done.2
  16.0 0.0 copy-done.3
  16.0 0.0 copy-done.4
  16.0 4.8 %shard_map.87 = (bf16[1792,384]{1,0:T(8,128)(2,1)S(1)}, bf16[384,1792]{1,0:T(8,128)(2,1)}, bf16[400,96]{1,0:T(8,128)(2,1)S(1)}, bf16[64,400]{1,0:T(8,128)(2,1)S(1)}, f32[400,128]{1,0:T(8,128)S(1)}) custom-call(f32[171,525]{1,0:T(8,128)S(1)} %copy-done, f32[21,400]{1,0:T(8,128)S(1)} %copy-done.1, f32[25,50]{1,0:T(8,128)S(1)} %copy-done.2, ...), custom_call_target="tpu_custom_call" | custom-call | flops 2000000000 | bytes 4000000 | tf_op jit(solution)/shard_map/pallas_call | solution.py:282
  20.8 5.9 %all-to-all-done.recv_ref = f32[8,219,128]{2,1,0:T(8,128)S(1)} async-done(((f32[8,219,128]{2,1,0:T(8,128)}), f32[8,219,128]{2,1,0:T(8,128)S(1)}, u32[]{:S(2)}, u32[]{:S(2)}) %all-to-all-start) | async-done | bytes 897056 | tf_op jit(solution)/shard_map/all_to_all | solution.py:403
  26.8 4.4 %all-to-all-start.2 = ((f32[8,171,128]{2,1,0:T(8,128)}), f32[8,171,128]{2,1,0:T(8,128)S(1)}, u32[]{:S(2)}, u32[]{:S(2)}) async-start(f32[8,171,128]{2,1,0:T(8,128)} %shard_map.89), calls=%async_computation.2 | async-start | bytes 1441792 | tf_op jit(solution)/shard_map/all_to_all | solution.py:405
  31.2 0.1 iota.7.owned_ref
  31.3 14.0 %shard_map.88 = f32[8,227,128]{2,1,0:T(8,128)} custom-call(s32[2,128]{1,0:T(2,128)S(1)} %iota.7.owned_ref, f32[8,219,128]{2,1,0:T(8,128)S(1)} %all-to-all-done.recv_ref, bf16[1792,384]{1,0:T(8,128)(2,1)S(1)} %get-tuple-element.9.refs_0_, bf16[384,1792]{1,0:T(8,128)(2,1)} %get-tuple-element.10.refs_1_, bf16[400,96]{1,0:T(8,128)(2,1)S(1)} %get-tuple-element.11.refs_2_, ...), custom_call_target="tpu_custom_call" | custom-call | flops 8000000000 | bytes 4000000 | tf_op jit(solution)/shard_map/pallas_call | solution.py:208
  45.3 0.0 all-to-all-done.2.recv_ref
  45.3 4.8 %all-to-all-start.1 = ((f32[8,227,128]{2,1,0:T(8,128)}), f32[8,227,128]{2,1,0:T(8,128)S(1)}, u32[]{:S(2)}, u32[]{:S(2)}) async-start(f32[8,227,128]{2,1,0:T(8,128)} %shard_map.88), calls=%async_computation.1 | async-start | bytes 1900544 | tf_op jit(solution)/shard_map/all_to_all | solution.py:408
  50.1 9.9 %shard_map.90 = f32[1,179,128]{2,1,0:T(8,128)S(1)} custom-call(s32[2,128]{1,0:T(2,128)S(1)} %iota.7.owned_ref, f32[8,171,128]{2,1,0:T(8,128)S(1)} %all-to-all-done.2.recv_ref, bf16[1792,384]{1,0:T(8,128)(2,1)S(1)} %get-tuple-element.9.refs_0_, bf16[384,1792]{1,0:T(8,128)(2,1)} %get-tuple-element.10.refs_1_, bf16[400,96]{1,0:T(8,128)(2,1)S(1)} %get-tuple-element.11.refs_2_, ...), custom_call_target="tpu_custom_call" | custom-call | flops 8000000000 | bytes 4000000 | tf_op jit(solution)/shard_map/pallas_call | solution.py:208
  60.0 14.0 %all_gather.3.b_ref = f32[8,179,128]{2,1,0:T(8,128)S(1)} all-gather(f32[1,179,128]{2,1,0:T(8,128)S(1)} %shard_map.90), channel_id=1, replica_groups=mesh['band'=8,'domain'=64] {'band'}, dimensions={0}, use_global_device_ids=true | all-gather | bytes 824832 | tf_op jit(solution)/shard_map/all_gather | solution.py:410
  74.1 0.0 all-to-all-done.1.a_ref
  74.1 1.3 %shard_map.91 = (f32[171,2304]{1,0:T(8,128)}, f32[18,128]{1,0:T(8,128)}) custom-call(f32[8,227,128]{2,1,0:T(8,128)S(1)} %all-to-all-done.1.a_ref, f32[8,179,128]{2,1,0:T(8,128)S(1)} %all_gather.3.b_ref), custom_call_target="tpu_custom_call" | custom-call | flops 100000000 | bytes 3000000 | tf_op jit(solution)/shard_map/pallas_call | solution.py:381
  (1 shorter events, 0.0 us)
Async XLA Ops:
  2.9 23.9 %all-to-all-start = ((f32[8,219,128]{2,1,0:T(8,128)}), f32[8,219,128]{2,1,0:T(8,128)S(1)}, u32[]{:S(2)}, u32[]{:S(2)}) async-start(f32[8,219,128]{2,1,0:T(8,128)} %shard_map.86), calls=%async_computation | async-start | bytes 1835008 | tf_op jit(solution)/shard_map/all_to_all | solution.py:403
  13.2 2.8 %copy-start = (f32[171,525]{1,0:T(8,128)S(1)}, f32[171,525]{1,0:T(8,128)}, u32[]{:S(2)}) copy-start(f32[171,525]{1,0:T(8,128)} %gaunt_ref.1) | copy-start | bytes 1077304
  13.2 2.8 %copy-start.1 = (f32[21,400]{1,0:T(8,128)S(1)}, f32[21,400]{1,0:T(8,128)}, u32[]{:S(2)}) copy-start(f32[21,400]{1,0:T(8,128)} %waves_ref.1) | copy-start | bytes 100804
  13.2 2.8 %copy-start.2 = (f32[25,50]{1,0:T(8,128)S(1)}, f32[25,50]{1,0:T(8,128)}, u32[]{:S(2)}) copy-start(f32[25,50]{1,0:T(8,128)} %y_ref.1) | copy-start | bytes 15004
  13.2 2.8 %copy-start.3 = (f32[400]{0:T(512)S(1)}, f32[400]{0:T(512)}, u32[]{:S(2)}) copy-start(f32[400]{0:T(512)} %param.12) | copy-start | bytes 4804
  13.2 2.8 %copy-start.4 = (f32[400]{0:T(512)S(1)}, f32[400]{0:T(512)}, u32[]{:S(2)}) copy-start(f32[400]{0:T(512)} %param.13) | copy-start | bytes 4804
  26.8 18.5 %all-to-all-start.2 = ((f32[8,171,128]{2,1,0:T(8,128)}), f32[8,171,128]{2,1,0:T(8,128)S(1)}, u32[]{:S(2)}, u32[]{:S(2)}) async-start(f32[8,171,128]{2,1,0:T(8,128)} %shard_map.89), calls=%async_computation.2 | async-start | bytes 1441792 | tf_op jit(solution)/shard_map/all_to_all | solution.py:405
  45.3 28.8 %all-to-all-start.1 = ((f32[8,227,128]{2,1,0:T(8,128)}), f32[8,227,128]{2,1,0:T(8,128)S(1)}, u32[]{:S(2)}, u32[]{:S(2)}) async-start(f32[8,227,128]{2,1,0:T(8,128)} %shard_map.88), calls=%async_computation.1 | async-start | bytes 1900544 | tf_op jit(solution)/shard_map/all_to_all | solution.py:408

commit v2 on v1

--- a/solution.py
+++ b/solution.py
@@ -39,7 +39,7 @@
     return energy, (points * (1.0 / square)) * (shifted * shifted + SLOPE_REST)
 
 
-def evaluate_blocks(pairs, part_of, b_ref, c_ref, e_ref, lhs_p_ref, lhs_b_ref, p_refs, v_refs):
+def evaluate_blocks(pairs, unroll, part_of, b_ref, c_ref, e_ref, lhs_p_ref, lhs_b_ref, p_refs, v_refs):
     grid_rows = lhs_p_ref.shape[0]
     cut = 208
     steps = [slice(0, 64), slice(64, 128), slice(128, 208), slice(208, 272), slice(272, 336), slice(336, 400)]
@@ -85,12 +85,12 @@
         p_refs[0][rows, :] = dot(lhs_p_ref[rows, :], rhs)
 
     def several(j, carry):
-        for i in range(4):
-            phase(4 * j + i, i % 2)
+        for i in range(unroll):
+            phase(unroll * j + i, i % 2)
         return carry
 
-    lax.fori_loop(0, pairs // 4, several, 0)
-    for g in range(pairs // 4 * 4, pairs):
+    lax.fori_loop(0, pairs // unroll, several, 0)
+    for g in range(pairs // unroll * unroll, pairs):
         phase(g, g % 2)
     finish(pairs - 1, v_refs[(pairs - 1) % 2])
 
@@ -180,7 +180,7 @@
         pairs = pairs + GROUP // 2
     e_ref[...] = jnp.zeros_like(e_ref)
     start_blocks(recv_ref, lives, mt, b_ref, directions)
-    evaluate_blocks(pairs, part_of, b_ref, c_ref, e_ref, lhs_p, lhs_b, (p0, p1), (v0, v1))
+    evaluate_blocks(pairs, 4 if narrow_base is None else 8, part_of, b_ref, c_ref, e_ref, lhs_p, lhs_b, (p0, p1), (v0, v1))
     energy = jnp.where(lives[0], energy_line(e_ref, 0, weight), 0.0)
     line = None
     if narrow_base is not None:

time: 75.8 us -> 75.2 us (level)
  transfers between devices with their start and end apart: 3 -> 3, of which waited for: 1 -> 1; matrix products, arithmetic and copies ran while one was open for 0% -> 0% of each run, Pallas kernels for 41% -> 40%
where the time goes in v2:
time: 75.2 us; the launch traced here: 74.8 us
  Pallas kernels  33.8 us (45%)
  starting transfers between devices  19.5 us (26%)
  blocking collectives  14 us (19%)
  waiting for transfers between devices  5.93 us (8%)
  between operations  1.45 us (2%)
    pallas_call x2, Pallas kernels, chunk_call(): pl.pallas_call(functools.partial(chunk_kernel, base, narrow_base, copies,...  23.3 us
    all_gather x1, blocking collectives, per_device(): all_b = lax.all_gather(out_b[0], 'band', axis=0)  14 us
    all_to_all x1, starting transfers between devices, per_device(): recv_a = lax.all_to_all(send_a, 'band', 0, 0, tiled=True)  10.3 us
    all_to_all x1, waiting for transfers between devices, per_device(): recv_a = lax.all_to_all(send_a, 'band', 0, 0, tiled=True)  5.93 us
    all_to_all x1, starting transfers between devices, per_device(): all_a = lax.all_to_all(out_a, 'band', 0, 0, tiled=True)  4.83 us
    pallas_call x1, Pallas kernels, make_tables(): pl.pallas_call(table_kernel, out_shape=(jax.ShapeDtypeStruct((rows, 2 * P...  4.8 us
    all_to_all x1, starting transfers between devices, per_device(): recv_b = lax.all_to_all(send_b, 'band', 0, 0, tiled=True)  4.41 us
    pallas_call x2, Pallas kernels, send_call(): pl.pallas_call(functools.partial(send_kernel, first, narrow), out_shape=p...  4.29 us
  transfers between devices with their start and end apart: 3, of which 1 were waited for; matrix products, arithmetic and copies ran while one was open for 0% of the time, Pallas kernels for 40%

profile of v2, /device:TPU:1, one launch (start us, length us, event | category | flops | bytes accessed | tf_op | source)
XLA Modules:
  0.0 74.8 jit_solution(11257300602132532468)
XLA Ops:
  0.6 2.2 %shard_map.86 = f32[8,219,128]{2,1,0:T(8,128)} custom-call(f32[171,1,2304]{2,1,0:T(1,128)} %bitcast.8), custom_call_target="tpu_custom_call" | custom-call | flops 100000000 | bytes 1500000 | tf_op jit(solution)/shard_map/pallas_call | solution.py:341
  2.9 10.3 %all-to-all-start = ((f32[8,219,128]{2,1,0:T(8,128)}), f32[8,219,128]{2,1,0:T(8,128)S(1)}, u32[]{:S(2)}, u32[]{:S(2)}) async-start(f32[8,219,128]{2,1,0:T(8,128)} %shard_map.86), calls=%async_computation | async-start | bytes 1835008 | tf_op jit(solution)/shard_map/all_to_all | solution.py:403
  13.2 0.0 copy-start
  13.2 0.0 copy-start.1
  13.2 0.0 copy-start.2
  13.2 0.0 copy-start.3
  13.2 0.0 copy-start.4
  13.9 2.0 %shard_map.89 = f32[8,171,128]{2,1,0:T(8,128)} custom-call(f32[171,1,2304]{2,1,0:T(1,128)} %bitcast.9), custom_call_target="tpu_custom_call" | custom-call | flops 100000000 | bytes 1500000 | tf_op jit(solution)/shard_map/pallas_call | solution.py:341
  16.0 0.0 copy-done
  16.0 0.0 copy-done.1
  16.0 0.0 copy-done.2
  16.0 0.0 copy-done.3
  16.0 0.0 copy-done.4
  16.0 4.8 %shard_map.87 = (bf16[1792,384]{1,0:T(8,128)(2,1)S(1)}, bf16[384,1792]{1,0:T(8,128)(2,1)}, bf16[400,96]{1,0:T(8,128)(2,1)S(1)}, bf16[64,400]{1,0:T(8,128)(2,1)S(1)}, f32[400,128]{1,0:T(8,128)S(1)}) custom-call(f32[171,525]{1,0:T(8,128)S(1)} %copy-done, f32[21,400]{1,0:T(8,128)S(1)} %copy-done.1, f32[25,50]{1,0:T(8,128)S(1)} %copy-done.2, ...), custom_call_target="tpu_custom_call" | custom-call | flops 2000000000 | bytes 4000000 | tf_op jit(solution)/shard_map/pallas_call | solution.py:282
  20.8 5.9 %all-to-all-done.recv_ref = f32[8,219,128]{2,1,0:T(8,128)S(1)} async-done(((f32[8,219,128]{2,1,0:T(8,128)}), f32[8,219,128]{2,1,0:T(8,128)S(1)}, u32[]{:S(2)}, u32[]{:S(2)}) %all-to-all-start) | async-done | bytes 897056 | tf_op jit(solution)/shard_map/all_to_all | solution.py:403
  26.8 4.4 %all-to-all-start.2 = ((f32[8,171,128]{2,1,0:T(8,128)}), f32[8,171,128]{2,1,0:T(8,128)S(1)}, u32[]{:S(2)}, u32[]{:S(2)}) async-start(f32[8,171,128]{2,1,0:T(8,128)} %shard_map.89), calls=%async_computation.2 | async-start | bytes 1441792 | tf_op jit(solution)/shard_map/all_to_all | solution.py:405
  31.2 0.1 iota.7.owned_ref
  31.3 13.4 %shard_map.88 = f32[8,227,128]{2,1,0:T(8,128)} custom-call(s32[2,128]{1,0:T(2,128)S(1)} %iota.7.owned_ref, f32[8,219,128]{2,1,0:T(8,128)S(1)} %all-to-all-done.recv_ref, bf16[1792,384]{1,0:T(8,128)(2,1)S(1)} %get-tuple-element.9.refs_0_, bf16[384,1792]{1,0:T(8,128)(2,1)} %get-tuple-element.10.refs_1_, bf16[400,96]{1,0:T(8,128)(2,1)S(1)} %get-tuple-element.11.refs_2_, ...), custom_call_target="tpu_custom_call" | custom-call | flops 8000000000 | bytes 4000000 | tf_op jit(solution)/shard_map/pallas_call | solution.py:208
  44.7 0.0 all-to-all-done.2.recv_ref
  44.7 4.8 %all-to-all-start.1 = ((f32[8,227,128]{2,1,0:T(8,128)}), f32[8,227,128]{2,1,0:T(8,128)S(1)}, u32[]{:S(2)}, u32[]{:S(2)}) async-start(f32[8,227,128]{2,1,0:T(8,128)} %shard_map.88), calls=%async_computation.1 | async-start | bytes 1900544 | tf_op jit(solution)/shard_map/all_to_all | solution.py:408
  49.5 9.9 %shard_map.90 = f32[1,179,128]{2,1,0:T(8,128)S(1)} custom-call(s32[2,128]{1,0:T(2,128)S(1)} %iota.7.owned_ref, f32[8,171,128]{2,1,0:T(8,128)S(1)} %all-to-all-done.2.recv_ref, bf16[1792,384]{1,0:T(8,128)(2,1)S(1)} %get-tuple-element.9.refs_0_, bf16[384,1792]{1,0:T(8,128)(2,1)} %get-tuple-element.10.refs_1_, bf16[400,96]{1,0:T(8,128)(2,1)S(1)} %get-tuple-element.11.refs_2_, ...), custom_call_target="tpu_custom_call" | custom-call | flops 8000000000 | bytes 4000000 | tf_op jit(solution)/shard_map/pallas_call | solution.py:208
  59.4 14.0 %all_gather.3.b_ref = f32[8,179,128]{2,1,0:T(8,128)S(1)} all-gather(f32[1,179,128]{2,1,0:T(8,128)S(1)} %shard_map.90), channel_id=1, replica_groups=mesh['band'=8,'domain'=64] {'band'}, dimensions={0}, use_global_device_ids=true | all-gather | bytes 824832 | tf_op jit(solution)/shard_map/all_gather | solution.py:410
  73.5 0.0 all-to-all-done.1.a_ref
  73.5 1.3 %shard_map.91 = (f32[171,2304]{1,0:T(8,128)}, f32[18,128]{1,0:T(8,128)}) custom-call(f32[8,227,128]{2,1,0:T(8,128)S(1)} %all-to-all-done.1.a_ref, f32[8,179,128]{2,1,0:T(8,128)S(1)} %all_gather.3.b_ref), custom_call_target="tpu_custom_call" | custom-call | flops 100000000 | bytes 3000000 | tf_op jit(solution)/shard_map/pallas_call | solution.py:381
  (1 shorter events, 0.0 us)
Async XLA Ops:
  2.9 23.9 %all-to-all-start = ((f32[8,219,128]{2,1,0:T(8,128)}), f32[8,219,128]{2,1,0:T(8,128)S(1)}, u32[]{:S(2)}, u32[]{:S(2)}) async-start(f32[8,219,128]{2,1,0:T(8,128)} %shard_map.86), calls=%async_computation | async-start | bytes 1835008 | tf_op jit(solution)/shard_map/all_to_all | solution.py:403
  13.2 2.8 %copy-start = (f32[171,525]{1,0:T(8,128)S(1)}, f32[171,525]{1,0:T(8,128)}, u32[]{:S(2)}) copy-start(f32[171,525]{1,0:T(8,128)} %gaunt_ref.1) | copy-start | bytes 1077304
  13.2 2.8 %copy-start.1 = (f32[21,400]{1,0:T(8,128)S(1)}, f32[21,400]{1,0:T(8,128)}, u32[]{:S(2)}) copy-start(f32[21,400]{1,0:T(8,128)} %waves_ref.1) | copy-start | bytes 100804
  13.2 2.8 %copy-start.2 = (f32[25,50]{1,0:T(8,128)S(1)}, f32[25,50]{1,0:T(8,128)}, u32[]{:S(2)}) copy-start(f32[25,50]{1,0:T(8,128)} %y_ref.1) | copy-start | bytes 15004
  13.2 2.8 %copy-start.3 = (f32[400]{0:T(512)S(1)}, f32[400]{0:T(512)}, u32[]{:S(2)}) copy-start(f32[400]{0:T(512)} %param.12) | copy-start | bytes 4804
  13.2 2.8 %copy-start.4 = (f32[400]{0:T(512)S(1)}, f32[400]{0:T(512)}, u32[]{:S(2)}) copy-start(f32[400]{0:T(512)} %param.13) | copy-start | bytes 4804
  26.8 17.9 %all-to-all-start.2 = ((f32[8,171,128]{2,1,0:T(8,128)}), f32[8,171,128]{2,1,0:T(8,128)S(1)}, u32[]{:S(2)}, u32[]{:S(2)}) async-start(f32[8,171,128]{2,1,0:T(8,128)} %shard_map.89), calls=%async_computation.2 | async-start | bytes 1441792 | tf_op jit(solution)/shard_map/all_to_all | solution.py:405
  44.7 28.8 %all-to-all-start.1 = ((f32[8,227,128]{2,1,0:T(8,128)}), f32[8,227,128]{2,1,0:T(8,128)S(1)}, u32[]{:S(2)}, u32[]{:S(2)}) async-start(f32[8,227,128]{2,1,0:T(8,128)} %shard_map.88), calls=%async_computation.1 | async-start | bytes 1900544 | tf_op jit(solution)/shard_map/all_to_all | solution.py:408

commit v3 on v2

--- a/solution.py
+++ b/solution.py
@@ -180,7 +180,7 @@
         pairs = pairs + GROUP // 2
     e_ref[...] = jnp.zeros_like(e_ref)
     start_blocks(recv_ref, lives, mt, b_ref, directions)
-    evaluate_blocks(pairs, 4 if narrow_base is None else 8, part_of, b_ref, c_ref, e_ref, lhs_p, lhs_b, (p0, p1), (v0, v1))
+    evaluate_blocks(pairs, 12 if narrow_base is None else 16, part_of, b_ref, c_ref, e_ref, lhs_p, lhs_b, (p0, p1), (v0, v1))
     energy = jnp.where(lives[0], energy_line(e_ref, 0, weight), 0.0)
     line = None
     if narrow_base is not None:

time: 75.2 us -> 75.1 us (level)
  no operation moved by 1% of the time
where the time goes in v3:
time: 75.1 us; the launch traced here: 74.7 us
  Pallas kernels  33.5 us (45%)
  starting transfers between devices  19.5 us (26%)
  blocking collectives  14 us (19%)
  waiting for transfers between devices  5.93 us (8%)
  between operations  1.61 us (2%)
    pallas_call x2, Pallas kernels, chunk_call(): pl.pallas_call(functools.partial(chunk_kernel, base, narrow_base, copies,...  23 us
    all_gather x1, blocking collectives, per_device(): all_b = lax.all_gather(out_b[0], 'band', axis=0)  14 us
    all_to_all x1, starting transfers between devices, per_device(): recv_a = lax.all_to_all(send_a, 'band', 0, 0, tiled=True)  10.3 us
    all_to_all x1, waiting for transfers between devices, per_device(): recv_a = lax.all_to_all(send_a, 'band', 0, 0, tiled=True)  5.92 us
    all_to_all x1, starting transfers between devices, per_device(): all_a = lax.all_to_all(out_a, 'band', 0, 0, tiled=True)  4.83 us
    pallas_call x1, Pallas kernels, make_tables(): pl.pallas_call(table_kernel, out_shape=(jax.ShapeDtypeStruct((rows, 2 * P...  4.81 us
    all_to_all x1, starting transfers between devices, per_device(): recv_b = lax.all_to_all(send_b, 'band', 0, 0, tiled=True)  4.41 us
    pallas_call x2, Pallas kernels, send_call(): pl.pallas_call(functools.partial(send_kernel, first, narrow), out_shape=p...  4.29 us
  transfers between devices with their start and end apart: 3, of which 1 were waited for; matrix products, arithmetic and copies ran while one was open for 0% of the time, Pallas kernels for 40%

profile of v3, /device:TPU:1, one launch (start us, length us, event | category | flops | bytes accessed | tf_op | source)
XLA Modules:
  0.0 74.7 jit_solution(17452581303013514395)
XLA Ops:
  0.6 2.2 %shard_map.86 = f32[8,219,128]{2,1,0:T(8,128)} custom-call(f32[171,1,2304]{2,1,0:T(1,128)} %bitcast.8), custom_call_target="tpu_custom_call" | custom-call | flops 100000000 | bytes 1500000 | tf_op jit(solution)/shard_map/pallas_call | solution.py:341
  2.9 10.3 %all-to-all-start = ((f32[8,219,128]{2,1,0:T(8,128)}), f32[8,219,128]{2,1,0:T(8,128)S(1)}, u32[]{:S(2)}, u32[]{:S(2)}) async-start(f32[8,219,128]{2,1,0:T(8,128)} %shard_map.86), calls=%async_computation | async-start | bytes 1835008 | tf_op jit(solution)/shard_map/all_to_all | solution.py:403
  13.2 0.0 copy-start
  13.2 0.0 copy-start.1
  13.2 0.0 copy-start.2
  13.2 0.0 copy-start.3
  13.2 0.0 copy-start.4
  13.9 2.0 %shard_map.89 = f32[8,171,128]{2,1,0:T(8,128)} custom-call(f32[171,1,2304]{2,1,0:T(1,128)} %bitcast.9), custom_call_target="tpu_custom_call" | custom-call | flops 100000000 | bytes 1500000 | tf_op jit(solution)/shard_map/pallas_call | solution.py:341
  16.0 0.0 copy-done
  16.0 0.0 copy-done.1
  16.0 0.0 copy-done.2
  16.0 0.0 copy-done.3
  16.0 0.0 copy-done.4
  16.0 4.8 %shard_map.87 = (bf16[1792,384]{1,0:T(8,128)(2,1)S(1)}, bf16[384,1792]{1,0:T(8,128)(2,1)}, bf16[400,96]{1,0:T(8,128)(2,1)S(1)}, bf16[64,400]{1,0:T(8,128)(2,1)S(1)}, f32[400,128]{1,0:T(8,128)S(1)}) custom-call(f32[171,525]{1,0:T(8,128)S(1)} %copy-done, f32[21,400]{1,0:T(8,128)S(1)} %copy-done.1, f32[25,50]{1,0:T(8,128)S(1)} %copy-done.2, ...), custom_call_target="tpu_custom_call" | custom-call | flops 2000000000 | bytes 4000000 | tf_op jit(solution)/shard_map/pallas_call | solution.py:282
  20.9 5.9 %all-to-all-done.recv_ref = f32[8,219,128]{2,1,0:T(8,128)S(1)} async-done(((f32[8,219,128]{2,1,0:T(8,128)}), f32[8,219,128]{2,1,0:T(8,128)S(1)}, u32[]{:S(2)}, u32[]{:S(2)}) %all-to-all-start) | async-done | bytes 897056 | tf_op jit(solution)/shard_map/all_to_all | solution.py:403
  26.8 4.4 %all-to-all-start.2 = ((f32[8,171,128]{2,1,0:T(8,128)}), f32[8,171,128]{2,1,0:T(8,128)S(1)}, u32[]{:S(2)}, u32[]{:S(2)}) async-start(f32[8,171,128]{2,1,0:T(8,128)} %shard_map.89), calls=%async_computation.2 | async-start | bytes 1441792 | tf_op jit(solution)/shard_map/all_to_all | solution.py:405
  31.2 0.1 iota.7.owned_ref
  31.3 13.3 %shard_map.88 = f32[8,227,128]{2,1,0:T(8,128)} custom-call(s32[2,128]{1,0:T(2,128)S(1)} %iota.7.owned_ref, f32[8,219,128]{2,1,0:T(8,128)S(1)} %all-to-all-done.recv_ref, bf16[1792,384]{1,0:T(8,128)(2,1)S(1)} %get-tuple-element.9.refs_0_, bf16[384,1792]{1,0:T(8,128)(2,1)} %get-tuple-element.10.refs_1_, bf16[400,96]{1,0:T(8,128)(2,1)S(1)} %get-tuple-element.11.refs_2_, ...), custom_call_target="tpu_custom_call" | custom-call | flops 8000000000 | bytes 4000000 | tf_op jit(solution)/shard_map/pallas_call | solution.py:208
  44.5 0.0 all-to-all-done.2.recv_ref
  44.5 4.8 %all-to-all-start.1 = ((f32[8,227,128]{2,1,0:T(8,128)}), f32[8,227,128]{2,1,0:T(8,128)S(1)}, u32[]{:S(2)}, u32[]{:S(2)}) async-start(f32[8,227,128]{2,1,0:T(8,128)} %shard_map.88), calls=%async_computation.1 | async-start | bytes 1900544 | tf_op jit(solution)/shard_map/all_to_all | solution.py:408
  49.4 9.8 %shard_map.90 = f32[1,179,128]{2,1,0:T(8,128)S(1)} custom-call(s32[2,128]{1,0:T(2,128)S(1)} %iota.7.owned_ref, f32[8,171,128]{2,1,0:T(8,128)S(1)} %all-to-all-done.2.recv_ref, bf16[1792,384]{1,0:T(8,128)(2,1)S(1)} %get-tuple-element.9.refs_0_, bf16[384,1792]{1,0:T(8,128)(2,1)} %get-tuple-element.10.refs_1_, bf16[400,96]{1,0:T(8,128)(2,1)S(1)} %get-tuple-element.11.refs_2_, ...), custom_call_target="tpu_custom_call" | custom-call | flops 8000000000 | bytes 4000000 | tf_op jit(solution)/shard_map/pallas_call | solution.py:208
  59.2 14.0 %all_gather.3.b_ref = f32[8,179,128]{2,1,0:T(8,128)S(1)} all-gather(f32[1,179,128]{2,1,0:T(8,128)S(1)} %shard_map.90), channel_id=1, replica_groups=mesh['band'=8,'domain'=64] {'band'}, dimensions={0}, use_global_device_ids=true | all-gather | bytes 824832 | tf_op jit(solution)/shard_map/all_gather | solution.py:410
  73.2 0.0 all-to-all-done.1.a_ref
  73.2 1.3 %shard_map.91 = (f32[171,2304]{1,0:T(8,128)}, f32[18,128]{1,0:T(8,128)}) custom-call(f32[8,227,128]{2,1,0:T(8,128)S(1)} %all-to-all-done.1.a_ref, f32[8,179,128]{2,1,0:T(8,128)S(1)} %all_gather.3.b_ref), custom_call_target="tpu_custom_call" | custom-call | flops 100000000 | bytes 3000000 | tf_op jit(solution)/shard_map/pallas_call | solution.py:381
  (1 shorter events, 0.0 us)
Async XLA Ops:
  2.9 23.9 %all-to-all-start = ((f32[8,219,128]{2,1,0:T(8,128)}), f32[8,219,128]{2,1,0:T(8,128)S(1)}, u32[]{:S(2)}, u32[]{:S(2)}) async-start(f32[8,219,128]{2,1,0:T(8,128)} %shard_map.86), calls=%async_computation | async-start | bytes 1835008 | tf_op jit(solution)/shard_map/all_to_all | solution.py:403
  13.2 2.8 %copy-start = (f32[171,525]{1,0:T(8,128)S(1)}, f32[171,525]{1,0:T(8,128)}, u32[]{:S(2)}) copy-start(f32[171,525]{1,0:T(8,128)} %gaunt_ref.1) | copy-start | bytes 1077304
  13.2 2.8 %copy-start.1 = (f32[21,400]{1,0:T(8,128)S(1)}, f32[21,400]{1,0:T(8,128)}, u32[]{:S(2)}) copy-start(f32[21,400]{1,0:T(8,128)} %waves_ref.1) | copy-start | bytes 100804
  13.2 2.8 %copy-start.2 = (f32[25,50]{1,0:T(8,128)S(1)}, f32[25,50]{1,0:T(8,128)}, u32[]{:S(2)}) copy-start(f32[25,50]{1,0:T(8,128)} %y_ref.1) | copy-start | bytes 15004
  13.2 2.8 %copy-start.3 = (f32[400]{0:T(512)S(1)}, f32[400]{0:T(512)}, u32[]{:S(2)}) copy-start(f32[400]{0:T(512)} %param.12) | copy-start | bytes 4804
  13.2 2.8 %copy-start.4 = (f32[400]{0:T(512)S(1)}, f32[400]{0:T(512)}, u32[]{:S(2)}) copy-start(f32[400]{0:T(512)} %param.13) | copy-start | bytes 4804
  26.8 17.8 %all-to-all-start.2 = ((f32[8,171,128]{2,1,0:T(8,128)}), f32[8,171,128]{2,1,0:T(8,128)S(1)}, u32[]{:S(2)}, u32[]{:S(2)}) async-start(f32[8,171,128]{2,1,0:T(8,128)} %shard_map.89), calls=%async_computation.2 | async-start | bytes 1441792 | tf_op jit(solution)/shard_map/all_to_all | solution.py:405
  44.5 28.7 %all-to-all-start.1 = ((f32[8,227,128]{2,1,0:T(8,128)}), f32[8,227,128]{2,1,0:T(8,128)S(1)}, u32[]{:S(2)}, u32[]{:S(2)}) async-start(f32[8,227,128]{2,1,0:T(8,128)} %shard_map.88), calls=%async_computation.1 | async-start | bytes 1900544 | tf_op jit(solution)/shard_map/all_to_all | solution.py:408
